TPU v7x, 256 devices: a whole 4x4x8 slice. The times are simulated.
256 devices in a mesh: group: 8 (over z), shard: 32 (over x, y, core).
Axes of the slice: x: 4, y: 4, z: 8, core: 2. Of those that a mesh axis runs over, the one named last changes fastest.
Arguments:
- queries: bfloat16 [1536, 1024], P(('group', 'shard')), may hold values from -12 to 12
- candidates: bfloat16 [1048576, 1024], P(('group', 'shard')), may hold values from -4 to 4
- targets: int32 [1536], replicated, may hold values from 0 to 1048575
Outputs:
- losses: float32 [1536], replicated
- mean_loss: float32 [], replicated
All inputs are finite; a program needn't handle non-finite values.
Results may differ from a plain program's by a relative error of at most 0.0003.
Values may be sent and summed in bfloat16 or wider, within the bound.
A program may use at most 64 MiB of HBM per device.

v0:
```python
import math

import jax
import jax.numpy as jnp
from jax import lax
from jax.sharding import Mesh
from jax.sharding import PartitionSpec as P

SHARD = ("shard_0", "shard_1", "shard_2")
GROUP_SHARD = ("group", "shard_0", "shard_1", "shard_2")


def laid_out(tiles, dim):
    shape = list(tiles.shape[1:])
    shape[dim] *= tiles.shape[0]
    return jnp.moveaxis(tiles, 0, dim).reshape(shape)


def gather_in_order(value, axes, order):
    tiles = value[None]
    for k in order:
        tiles = lax.all_gather(tiles, axes[k], axis=0, tiled=True)
    held = [lax.axis_size(axes[k]) for k in reversed(order)]
    tiles = tiles.reshape(*held, *value.shape)
    turned = sorted(range(len(order)), key=lambda place: order[len(order) - 1 - place])
    return tiles.transpose(*turned, *range(len(order), tiles.ndim)).reshape(-1, *value.shape)


def gather_axes(value, axes, order, dim):
    return laid_out(gather_in_order(value, axes, order), dim)


def from_everyone(value, axis):
    copies = jnp.broadcast_to(value, (lax.axis_size(axis), *value.shape))
    return lax.all_to_all(copies, axis, split_axis=0, concat_axis=0, tiled=True)


def collected_together(value, axis):
    leaves = jax.tree.leaves(value)
    order = sorted(range(len(leaves)), key=lambda k: -leaves[k].size)
    width = (1, *leaves[order[0]].shape)[-1]
    lines = [
        jnp.pad(leaves[k].reshape(-1), (0, -leaves[k].size % width)).reshape(-1, width)
        for k in order
    ]
    both, at, found = (from_everyone(jnp.concatenate(lines), axis), 0, {})
    for k, line in zip(order, lines):
        share = both[:, at : at + len(line)].reshape(len(both), -1)
        found[k] = share[:, : leaves[k].size].reshape(-1, *leaves[k].shape)
        at += len(line)
    numbers = iter(range(len(leaves)))
    return jax.tree.map(lambda _: found[next(numbers)], value)


def folded_in_pairs(pieces, combine):
    while len(jax.tree.leaves(pieces)[0]) > 1:
        pieces = jax.vmap(combine)(
            *(jax.tree.map(lambda part: part[side::2], pieces) for side in (0, 1))
        )
    return jax.tree.map(lambda part: part[0], pieces)


def combined_all(value, axis, combine):
    pieces = collected_together(value, axis)
    return folded_in_pairs(pieces, combine)


def once_a_type(value, axis):
    leaves, found = (jax.tree.leaves(value), {})
    for leading, a in enumerate(leaves):
        if leading not in found:
            alike = [k for k, b in enumerate(leaves) if b.dtype == a.dtype]
            got = (
                collected_together([leaves[k] for k in alike], axis)
                if len(alike) > 1
                else [from_everyone(a, axis)]
            )
            for k, b in zip(alike, got):
                found[k] = b
    numbers = iter(range(len(leaves)))
    return jax.tree.map(lambda _: found[next(numbers)], value)


def merged(value, axis, combine):
    pieces = once_a_type(value, axis)
    return folded_in_pairs(pieces, combine)


def combine(first, second):
    top = jnp.maximum(first[0], second[0])
    total = first[1] * jnp.exp(first[0] - top) + second[1] * jnp.exp(second[0] - top)
    return (top, total, first[2] + second[2])


def score_rows(piece, candidates, chosen_targets, owner):
    rows = candidates.shape[0]
    local = chosen_targets - owner * rows
    owned = (local >= 0) & (local < rows)
    chosen = jnp.take(candidates, jnp.clip(local, 0, rows - 1), axis=0)
    products = jnp.sum(piece.astype(jnp.float32) * chosen.astype(jnp.float32), axis=1)
    picked = jnp.where(owned, products, jnp.float32(0.0))
    count = piece.shape[0]
    block = math.gcd(count, 512)
    panels = piece.reshape(count // block, block, piece.shape[1])

    def score_panel(panel):
        scores = jnp.dot(panel, candidates.T, preferred_element_type=jnp.float32)
        peak = jnp.max(scores, axis=1)
        return (peak, jnp.sum(jnp.exp(scores - peak[:, None]), axis=1))

    peaks, sums = lax.map(score_panel, panels)
    return (peaks.reshape(count), sums.reshape(count), picked)


def on_device(queries, candidates, targets):
    owner = lax.axis_index("group") * lax.axis_size(SHARD) + lax.axis_index(SHARD)
    every = gather_axes(queries, GROUP_SHARD, (1, 0, 2, 3), 0)
    top, total, picked = score_rows(every, candidates, targets, owner)
    inner = combined_all((top, total, picked), SHARD, combine)
    top, total, picked = merged(inner, "group", combine)
    losses = top + jnp.log(total) - picked
    return (losses, jnp.mean(losses))


def solution(mesh):
    finer = Mesh(
        mesh.devices.reshape(mesh.shape["group"], 4, 4, 2),
        ("group", "shard_0", "shard_1", "shard_2"),
    )
    in_specs = (P(GROUP_SHARD, None), P(GROUP_SHARD, None), P())
    out_specs = (P(), P())
    return jax.shard_map(
        on_device, mesh=finer, in_specs=in_specs, out_specs=out_specs, check_vma=False
    )
```

profile of v0, /device:TPU:1, one launch (start us, length us, event | category | flops | bytes accessed | tf_op | source)
XLA Modules:
  0.0 195.4 jit_solution(15849809175005774843)
XLA Ops:
  7.2 0.0 all-gather.5.cloned.1.call-start
  7.2 10.4 %all-gather.1 = bf16[4,6,1024]{2,1,0:T(8,128)(2,1)S(1)} all-gather(bf16[1,6,1024]{2,1,0:T(8,128)(2,1)} %bitcast.56), channel_id=2, replica_groups=mesh['group'=8,'shard_0'=4,'shard_1'=4,'shard_2'=2] {'shard_0'}, dimensions={0}, use_global_device_ids=true | all-gather | bytes 61440 | tf_op jit(solution)/shard_map/all_gather | solution.py:22
  17.6 23.3 %all_gather.13 = bf16[32,6,1024]{2,1,0:T(8,128)(2,1)S(1)} all-gather(bf16[4,6,1024]{2,1,0:T(8,128)(2,1)S(1)} %all-gather.1), channel_id=1, replica_groups=mesh['group'=8,'shard_0'=4,'shard_1'=4,'shard_2'=2] {'group'}, dimensions={0}, use_global_device_ids=true | all-gather | bytes 442368 | tf_op jit(solution)/shard_map/all_gather | solution.py:22
  40.9 1.0 copy.36
  41.8 0.0 all-gather.5.cloned.1.call-update
  41.9 0.0 all-gather.7.cloned.1.call-start
  41.9 36.5 %all-gather.5.cloned.1.call-done = bf16[128,6,1024]{2,0,1:T(8,128)(2,1)} async-done(((bf16[32,6,1024]{2,0,1:T(8,128)(2,1)}), bf16[128,6,1024]{2,0,1:T(8,128)(2,1)}) %all-gather.5.cloned.1.call-update) | async-done | bytes 1572880 | tf_op jit(solution)/shard_map/all_gather | solution.py:22
  78.4 0.0 all-gather.7.cloned.1.call-update
  78.5 0.7 compare_and_fusion
  79.2 11.6 %gather_fusion = bf16[1536,1024]{1,0:T(8,128)(2,1)S(1)} fusion(bf16[4096,1024]{1,0:T(8,128)(2,1)} %param.6, s32[2048]{0:T(1024)S(1)} %pad_clamp_fusion), kind=kCustom, calls=%fused_computation | custom fusion | bytes 6297600 | tf_op jit(solution)/shard_map/jit(_take)/gather | solution.py:99
  90.8 2.9 %gather.7 = bf16[8,4,4,2,6,1024]{5,4,3,2,1,0:T(8,128)(2,1)} reshape(bf16[1536,1024]{1,0:T(8,128)(2,1)S(1)} %gather_fusion) | data formatting | bytes 6291456 | tf_op jit(solution)/shard_map/jit(_take)/gather | solution.py:99
  93.7 0.2 broadcast_in_dim.36
  93.9 0.6 copy.38
  94.5 4.1 %all-gather.7.cloned.1.call-done = bf16[256,6,1024]{2,0,1:T(8,128)(2,1)} async-done(((bf16[128,6,1024]{2,0,1:T(8,128)(2,1)}), bf16[256,6,1024]{2,0,1:T(8,128)(2,1)}) %all-gather.7.cloned.1.call-update) | async-done | bytes 3145744 | tf_op jit(solution)/shard_map/all_gather | solution.py:22
  98.6 4.0 %reshape.57 = bf16[2,4,8,4,6,1024]{5,3,2,1,0,4:T(4,128)(2,1)S(1)} reshape(bf16[256,6,1024]{2,0,1:T(8,128)(2,1)} %all-gather.7.cloned.1.call-done) | data formatting | bytes 6291456 | tf_op jit(solution)/shard_map/reshape | solution.py:24
  102.6 0.0 copy-start
  102.6 7.8 %multiply_reduce_fusion = f32[8,4,4,2,6]{1,0,2,3,4:T(8,128)S(1)} fusion(bf16[8,4,4,2,6,1024]{5,4,3,2,1,0:T(8,128)(2,1)} %gather.7, pred[8,4,4,2,6]{1,0,2,3,4:T(8,128)(4,1)S(1)} %copy.38, bf16[2,4,8,4,6,1024]{5,3,2,1,0,4:T(4,128)(2,1)S(1)} %reshape.57), kind=kLoop, calls=%fused_computation.6 | loop fusion | flops 7862784 | bytes 6299136 | tf_op jit(solution)/shard_map/reduce_sum | solution.py:100
  110.4 0.5 copy.40
  111.0 0.2 reduce_sum.30
  111.2 0.0 copy-done
  111.2 3.7 %copy.37 = bf16[8,4,4,2,6,1024]{5,4,3,2,1,0:T(8,128)(2,1)} copy(bf16[8,4,4,2,6,1024]{5,1,0,2,3,4:T(4,128)(2,1)S(1)} %bitcast.43) | data formatting | bytes 6291456 | tf_op jit(solution)/shard_map/transpose | solution.py:26
  115.0 4.9 %reshape_reshape_reshape.3 = bf16[3,512,1024]{2,1,0:T(8,128)(2,1)S(1)} reshape(bf16[8,4,4,2,6,1024]{5,4,3,2,1,0:T(8,128)(2,1)} %copy.37) | data formatting | bytes 6291456 | tf_op jit(solution)/shard_map/reshape;reshape;reshape | solution.py:104
  119.8 25.6 %while.12 = (s32[]{:T(128)}, f32[3,512]{1,0:T(4,128)S(1)}, f32[3,512]{1,0:T(4,128)S(1)}, bf16[3,512,1024]{2,1,0:T(8,128)(2,1)S(1)}, bf16[4096,1024]{1,0:T(8,128)(2,1)}, /*index=5*/s32[]{:T(128)}, s32[]{:T(128)}) while((s32[]{:T(128)}, f32[3,512]{1,0:T(4,128)S(1)}, f32[3,512]{1,0:T(4,128)S(1)}, bf16[3,512,1024]{2,1,0:T(8,128)(2,1)S(1)}, ...), condition=%wide.region_3.4_spmd, body=%wide.region_0.0_spmd.sunk | while | flops 4301257728 | bytes 26228824 | solution.py:111
  119.9 7.1 %fusion.16 = (f32[512]{0:T(512)S(1)}, f32[512,4096]{1,0:T(8,128)S(1)}) fusion(bf16[4096,1024]{1,0:T(8,128)(2,1)} %get-tuple-element.123, bf16[3,512,1024]{2,1,0:T(8,128)(2,1)S(1)} %get-tuple-element.122, s32[]{:T(128)} %get-tuple-element.112), kind=kOutput, calls=%fused_computation.39.clone.1 | convolution fusion | flops 4297063936 | bytes 17827844 | tf_op jit(solution)/shard_map/while/body/eval_jaxpr/dot_general | solution.py:107
  127.0 1.3 exponential_reduce_fusion.2
  128.3 0.1 dynamic_update_slice.9
  128.4 7.1 %fusion.16 = (f32[512]{0:T(512)S(1)}, f32[512,4096]{1,0:T(8,128)S(1)}) fusion(bf16[4096,1024]{1,0:T(8,128)(2,1)} %get-tuple-element.123, bf16[3,512,1024]{2,1,0:T(8,128)(2,1)S(1)} %get-tuple-element.122, s32[]{:T(128)} %get-tuple-element.112), kind=kOutput, calls=%fused_computation.39.clone.1 | convolution fusion | flops 4297063936 | bytes 17827844 | tf_op jit(solution)/shard_map/while/body/eval_jaxpr/dot_general | solution.py:107
  135.5 1.3 exponential_reduce_fusion.2
  136.8 0.1 dynamic_update_slice.9
  136.9 7.1 %fusion.16 = (f32[512]{0:T(512)S(1)}, f32[512,4096]{1,0:T(8,128)S(1)}) fusion(bf16[4096,1024]{1,0:T(8,128)(2,1)} %get-tuple-element.123, bf16[3,512,1024]{2,1,0:T(8,128)(2,1)S(1)} %get-tuple-element.122, s32[]{:T(128)} %get-tuple-element.112), kind=kOutput, calls=%fused_computation.39.clone.1 | convolution fusion | flops 4297063936 | bytes 17827844 | tf_op jit(solution)/shard_map/while/body/eval_jaxpr/dot_general | solution.py:107
  144.0 1.3 exponential_reduce_fusion.2
  145.4 0.1 dynamic_update_slice.9
  145.5 0.1 broadcast_in_dim.41
  145.6 20.8 %all_to_all.10 = f32[32,3,1536]{2,1,0:T(4,128)S(1)} all-to-all(f32[32,3,1536]{2,1,0:T(4,128)S(1)} %broadcast_in_dim.41), channel_id=1, replica_groups=mesh['group'=8,'shard_0'=4,'shard_1'=4,'shard_2'=2] {'shard_0','shard_1'..., dimensions={0} | all-to-all | bytes 1179648 | tf_op jit(solution)/shard_map/all_to_all | solution.py:35
  166.5 0.4 fusion.10
  168.0 17.4 %all_to_all.11 = f32[8,3,1536]{2,1,0:T(4,128)S(1)} all-to-all(f32[8,3,1536]{2,1,0:T(4,128)S(1)} %broadcast_in_dim.42), channel_id=1, replica_groups=mesh['group'=8,'shard_0'=4,'shard_1'=4,'shard_2'=2] {'group'}, dimensions={0} | all-to-all | bytes 294912 | tf_op jit(solution)/shard_map/all_to_all | solution.py:35
  185.5 0.1 fusion.11
  186.0 0.7 fusion.8
  (68 shorter events, 1.6 us)
Async XLA Ops:
  7.2 71.3 %all-gather.5.cloned.1.call-start = ((), (), s32[]{:S(2)}) async-start(), calls=%async_computation.2 | async-start | bytes 1966080 | tf_op jit(solution)/shard_map/all_gather | solution.py:22
  41.9 56.7 %all-gather.7.cloned.1.call-start = ((), (), s32[]{:S(2)}) async-start(), calls=%async_computation.3 | async-start | bytes 4718592 | tf_op jit(solution)/shard_map/all_gather | solution.py:22
  102.6 8.6 %copy-start = (s32[1536]{0:T(1024)S(1)}, s32[1536]{0:T(1024)}, u32[]{:S(2)}) copy-start(s32[1536]{0:T(1024)} %param.7) | copy-start | bytes 18436
Sparse Core Ops, SparseCore 0:
  42.0 36.4 all-gather.4
  80.2 18.3 all-gather.6
where the time goes:
time: 196 us; the launch traced here: 195 us
  blocking collectives  71.9 us (37%)
  waiting for transfers between devices  40.6 us (21%)
  local copies, waits for them, and re-layouts  31.7 us (16%)
  matrix products  21.4 us (11%)
  between operations  16.2 us (8%)
  other arithmetic  13.4 us (7%)
    all_gather x2, waiting for transfers between devices, gather_in_order(): tiles = lax.all_gather(tiles, axes[k], axis=0, tiled=True)  40.6 us
    all_to_all x2, blocking collectives, from_everyone(): return lax.all_to_all(copies, axis, split_axis=0, concat_axis=0, tiled=True)  38.3 us
    all_gather x2, blocking collectives, gather_in_order(): tiles = lax.all_gather(tiles, axes[k], axis=0, tiled=True)  33.7 us
    dot_general x3, matrix products, score_panel(): scores = jnp.dot(panel, candidates.T, preferred_element_type=jnp.float32)  21.4 us
    gather x2, local copies, waits for them, and re-layouts, score_rows(): chosen = jnp.take(candidates, jnp.clip(local, 0, rows - 1), axis=0)  14.5 us
    reduce_sum x1, other arithmetic, score_rows(): jnp.sum(piece.astype(jnp.float32) * chosen.astype(jnp.float32), axis=1)  7.8 us
    another operation x1, local copies, waits for them, and re-layouts, score_rows(): panels = piece.reshape(count // block, block, piece.shape[1])  4.87 us
    reshape x1, local copies, waits for them, and re-layouts, gather_in_order(): tiles = tiles.reshape(*held, *value.shape)  4.01 us
  transfers between devices with their start and end apart: 2, of which 2 were waited for; matrix products, arithmetic and copies ran while one was open for 8% of the time, Pallas kernels for 0%

commit v1 on v0

v1 whole, which is shorter than its diff:
```python
import functools

import jax
import jax.numpy as jnp
from jax import lax
from jax.experimental import pallas as pl
from jax.experimental.pallas import tpu as pltpu
from jax.sharding import PartitionSpec as P

F32 = jnp.float32
BF16 = jnp.bfloat16
MESH = pl.DeviceIdType.MESH
LOW = -3.0e38
PER = 6
BLOCK = 48
UNIT = 192
OWN = {0: 0, 1: 2, 3: 3, 2: 6}
OTHER = {0: 1, 1: 4, 3: 5, 2: 7}
NEAR_FIRST = (1, 3, 2)


def place():
    z = lax.axis_index("group")
    s = lax.axis_index("shard")
    x, y, c = s // 8, (s // 2) % 4, s % 2
    u = y * (1 - c) + x * c
    v = x * (1 - c) + y * c
    return z, u, v, c


def at(z, u, v, c):
    x = v * (1 - c) + u * c
    y = u * (1 - c) + v * c
    return (z, (x * 4 + y) * 2 + c)


def rows_of(slot, v):
    return pl.ds(pl.multiple_of(slot * UNIT + v * BLOCK, 16), BLOCK)


def meet(others):
    barrier = pltpu.get_barrier_semaphore()
    for other in others:
        pl.semaphore_signal(barrier, inc=1, device_id=other, device_id_type=MESH)
    pl.semaphore_wait(barrier, len(others))


def gather_kernel(q_ref, all_ref, first, send1, recv1, send2, recv2, send3, recv3, sendp, recvp):
    z, u, v, c = place()
    partner = (z, at(z, u, v, c)[1] + 1 - 2 * c)
    column = [at((z + d) % 8, u, v, c) for d in range(1, 8)]
    along_v = {d: at(z, u, (v + d) % 4, c) for d in NEAR_FIRST}
    along_u = {d: at(z, (u + d) % 4, v, c) for d in NEAR_FIRST}
    meet(column + list(along_v.values()) + list(along_u.values()) + [partner])

    def copy(src, dst, send, recv, to):
        return pltpu.make_async_remote_copy(
            src_ref=src, dst_ref=dst, send_sem=send, recv_sem=recv, device_id=to, device_id_type=MESH
        )

    first[z] = q_ref[...]
    sent = []
    for d in (4, 3, 5, 2, 6, 1, 7):
        one = copy(q_ref, first.at[z], send1.at[d], recv1.at[d], column[d - 1])
        one.start()
        sent.append(one)
    for d in (1, 7, 2, 6, 3, 5, 4):
        here = first.at[(z + 8 - d) % 8]
        copy(here, here, send1.at[d], recv1.at[d], column[d - 1]).wait_recv()
    block = jnp.concatenate([first[k].astype(F32) for k in range(8)], axis=0)
    all_ref[rows_of(0, v), :] = block.astype(BF16)

    def pass_on(d):
        src = (v + 4 - d) % 4
        held = all_ref.at[rows_of(0, src)]
        to = [(held, OTHER[0], sendp.at[0, d], recvp.at[0, d], partner)]
        for e in NEAR_FIRST:
            to.append((held, OWN[(4 - e) % 4], send3.at[e, d], recv3.at[e, d], along_u[e]))
        for held, slot, send, recv, device in to:
            one = copy(held, all_ref.at[rows_of(slot, src)], send, recv, device)
            one.start()
            sent.append(one)

    own = all_ref.at[rows_of(0, v)]
    for d in NEAR_FIRST:
        one = copy(own, own, send2.at[d], recv2.at[d], along_v[d])
        one.start()
        sent.append(one)
    pass_on(0)
    for d in NEAR_FIRST:
        here = all_ref.at[rows_of(0, (v + 4 - d) % 4)]
        copy(here, here, send2.at[d], recv2.at[d], along_v[d]).wait_recv()
        pass_on(d)
    for d in (0, 1, 3, 2):
        for e in NEAR_FIRST:
            far = (4 - e) % 4
            src = (v + 4 - d) % 4
            here = all_ref.at[rows_of(OWN[far], src)]
            copy(here, here, send3.at[e, d], recv3.at[e, d], along_u[e]).wait_recv()
            one = copy(here, all_ref.at[rows_of(OTHER[far], src)], sendp.at[far, d], recvp.at[far, d], partner)
            one.start()
            sent.append(one)
    for far in (0, 1, 3, 2):
        for d in range(4):
            here = all_ref.at[rows_of(OTHER[far], (u + 4 - d) % 4)]
            copy(here, here, sendp.at[far, d], recvp.at[far, d], partner).wait_recv()
    for one in sent:
        one.wait_send()


def gather(queries):
    dma = pltpu.SemaphoreType.DMA
    return pl.pallas_call(
        gather_kernel,
        out_shape=jax.ShapeDtypeStruct((8 * UNIT, queries.shape[1]), BF16),
        in_specs=[pl.BlockSpec(memory_space=pltpu.VMEM)],
        out_specs=pl.BlockSpec(memory_space=pltpu.VMEM),
        scratch_shapes=[pltpu.VMEM((8, PER, queries.shape[1]), BF16)]
        + [dma((8,)), dma((8,)), dma((4,)), dma((4,)), dma((4, 4)), dma((4, 4)), dma((4, 4)), dma((4, 4))],
        compiler_params=pltpu.CompilerParams(collective_id=1, has_side_effects=True),
        name="gather_queries",
    )(queries)


def score_kernel(rows, cols, q_ref, c_hbm, t_ref, o_ref, c_buf, s0, s1, sem):
    count = c_buf.shape[0]
    blocks = count // rows
    chunk = 1024
    loads = [
        pltpu.make_async_copy(c_hbm.at[pl.ds(i * chunk, chunk)], c_buf.at[pl.ds(i * chunk, chunk)], sem.at[i])
        for i in range(count // chunk)
    ]
    for load in loads:
        load.start()
    for load in loads:
        load.wait()
    groups = rows // 8
    z, u, v, c = place()

    def scored(q, k):
        part = c_buf[pl.ds(pl.multiple_of(k * rows, rows), rows), :]
        return lax.dot_general(part, q, (((1,), (1,)), ((), ())), preferred_element_type=F32)

    def peak(scores, top):
        return jnp.maximum(top, jnp.max(scores.reshape(groups, 8, cols), axis=0))

    results = []
    for batch in range(q_ref.shape[0] // cols):
        q_rows = pl.ds(batch * cols, cols)
        wanted = jnp.broadcast_to(t_ref[:, batch * cols : (batch + 1) * cols], (8, cols))
        wanted = wanted - lax.broadcasted_iota(jnp.int32, (8, cols), 0)

        def take(held, k, old, new, total, picked, wanted=wanted):
            total = total * jnp.exp(old - new)
            for g in range(groups):
                value = held[g * 8 : (g + 1) * 8, :]
                total = total + jnp.exp(value - new)
                picked = jnp.where(wanted == k * rows + g * 8, value, picked)
            return total, picked

        def step(j, carry, q_rows=q_rows, take=take):
            old, new, total, picked = carry
            scores = scored(q_ref[q_rows, :], 2 * j + 1)
            s1[...] = scores
            newer = peak(scores, new)
            total, picked = take(s0, 2 * j, old, new, total, picked)
            scores = scored(q_ref[q_rows, :], 2 * j + 2)
            s0[...] = scores
            newest = peak(scores, newer)
            total, picked = take(s1, 2 * j + 1, new, newer, total, picked)
            return newer, newest, total, picked

        old = jnp.full((8, cols), LOW, F32)
        zero = jnp.zeros((8, cols), F32)
        scores = scored(q_ref[q_rows, :], 0)
        s0[...] = scores
        carry = (old, peak(scores, old), zero, zero)
        old, new, total, picked = lax.fori_loop(0, blocks // 2 - 1, step, carry)
        scores = scored(q_ref[q_rows, :], blocks - 1)
        s1[...] = scores
        newer = peak(scores, new)
        total, picked = take(s0, blocks - 2, old, new, total, picked)
        total, picked = take(s1, blocks - 1, new, newer, total, picked)
        top = jnp.max(newer, axis=0, keepdims=True)
        total = jnp.sum(total * jnp.exp(newer - top), axis=0, keepdims=True)
        results.append((top, total, jnp.sum(picked, axis=0, keepdims=True)))
    lines = [jnp.concatenate(parts, axis=1) for parts in zip(*results)]
    for far in range(4):
        for slot, unit in ((OWN[far], c * 4 + (u + far) % 4), (OTHER[far], (1 - c) * 4 + (v + far) % 4)):
            parts = []
            for line in lines:
                parts.append(line[:, slot * UNIT : slot * UNIT + 128])
                parts.append(line[:, slot * UNIT + 64 : slot * UNIT + 192])
            o_ref[unit] = jnp.concatenate(parts + [jnp.zeros((2, 128), F32)], axis=0)


def score(queries, candidates, targets, rows=512, cols=512):
    count, width = candidates.shape
    return pl.pallas_call(
        functools.partial(score_kernel, rows, cols),
        out_shape=jax.ShapeDtypeStruct((8, 8, 128), F32),
        in_specs=[
            pl.BlockSpec(memory_space=pltpu.VMEM),
            pl.BlockSpec(memory_space=pl.ANY),
            pl.BlockSpec(memory_space=pltpu.VMEM),
        ],
        out_specs=pl.BlockSpec(memory_space=pltpu.VMEM),
        scratch_shapes=[
            pltpu.VMEM((count, width), BF16),
            pltpu.VMEM((rows, cols), F32),
            pltpu.VMEM((rows, cols), F32),
            pltpu.SemaphoreType.DMA((count // 1024,)),
        ],
        compiler_params=pltpu.CompilerParams(vmem_limit_bytes=50 << 20),
        name="score_queries",
    )(queries, candidates, targets)


def combined(tiles):
    tops = [tile[0:2] for tile in tiles]
    top = functools.reduce(jnp.maximum, tops)
    total = sum(tile[2:4] * jnp.exp(one - top) for tile, one in zip(tiles, tops))
    picked = sum(tile[4:6] for tile in tiles)
    return jnp.concatenate([top, total, picked, jnp.zeros((2, 128), F32)], axis=0)


def reduce_kernel(r_ref, o_ref, from_core, at_x, from_x, at_y, from_y, at_z, from_z, mine, sends, recvs):
    z = lax.axis_index("group")
    s = lax.axis_index("shard")
    x, y, c = s // 8, (s // 2) % 4, s % 2

    def device(z, x, y, c):
        return (z, (x * 4 + y) * 2 + c)

    partner = device(z, x, y, 1 - c)
    xs = [device(z, (x + d) % 4, y, c) for d in range(1, 4)]
    crossed = [device(z, (x + d) % 4, y, 1 - c) for d in range(1, 4)]
    ys = [device(z, x, (y + d) % 4, c) for d in range(1, 4)]
    zs = [device((z + d) % 8, x, y, c) for d in range(1, 8)]
    meet([partner] + xs + crossed + ys + zs)

    def copy(k, src, dst, to):
        return pltpu.make_async_remote_copy(
            src_ref=src, dst_ref=dst, send_sem=sends.at[k], recv_sem=recvs.at[k], device_id=to, device_id_type=MESH
        )

    half = pl.ds((1 - c) * 4, 4)
    one = copy(0, r_ref.at[half], from_core, partner)
    one.start()
    sent = [one]
    one.wait_recv()
    for k in range(4):
        at_x[k] = combined([r_ref[c * 4 + k], from_core[k]])
    for d in range(1, 4):
        one = copy(d, at_x.at[(x + d) % 4], from_x.at[d], xs[d - 1])
        one.start()
        sent.append(one)
    for one in sent[1:4]:
        one.wait_recv()
    at_y[...] = combined([at_x[x]] + [from_x[d] for d in range(1, 4)])
    for d in range(1, 4):
        one = copy(3 + d, at_y, from_y.at[d], ys[d - 1])
        one.start()
        sent.append(one)
    for one in sent[4:7]:
        one.wait_recv()
    at_z[...] = combined([at_y[...]] + [from_y[d] for d in range(1, 4)])
    for d in (4, 3, 5, 2, 6, 1, 7):
        one = copy(6 + d, at_z, from_z.at[d], zs[d - 1])
        one.start()
        sent.append(one)
    for one in sent[7:14]:
        one.wait_recv()
    whole = combined([at_z[...]] + [from_z[d] for d in range(1, 8)])
    loss = whole[0:2] + jnp.log(whole[2:4]) - whole[4:6]
    mine[...] = jnp.concatenate([loss, jnp.zeros((6, 128), F32)], axis=0)
    unit = c * 4 + x
    o_ref[unit] = mine[...]
    for d in range(7):
        one = copy(14 + d, mine, o_ref.at[unit], ([partner] + xs + crossed)[d])
        one.start()
        sent.append(one)
    for d in range(7):
        other = c * 4 if 1 <= d < 4 else (1 - c) * 4
        here = o_ref.at[other + (x + 4 - (0, 1, 2, 3, 1, 2, 3)[d]) % 4]
        copy(14 + d, mine, here, partner).wait_recv()
    for one in sent:
        one.wait_send()


def reduced(partial):
    tile = (8, 128)
    dma = pltpu.SemaphoreType.DMA
    return pl.pallas_call(
        reduce_kernel,
        out_shape=jax.ShapeDtypeStruct((8, *tile), F32),
        in_specs=[pl.BlockSpec(memory_space=pltpu.VMEM)],
        out_specs=pl.BlockSpec(memory_space=pltpu.VMEM),
        scratch_shapes=[
            pltpu.VMEM((4, *tile), F32),
            pltpu.VMEM((4, *tile), F32),
            pltpu.VMEM((4, *tile), F32),
            pltpu.VMEM(tile, F32),
            pltpu.VMEM((4, *tile), F32),
            pltpu.VMEM(tile, F32),
            pltpu.VMEM((8, *tile), F32),
            pltpu.VMEM(tile, F32),
            dma((21,)),
            dma((21,)),
        ],
        compiler_params=pltpu.CompilerParams(collective_id=2, has_side_effects=True),
        name="reduce_losses",
    )(partial)


def in_place_order(targets):
    t = targets.reshape(8, 4, 4, 2, PER)
    low = t[:, :, :, 0].transpose(2, 1, 0, 3).reshape(4, UNIT)
    high = t[:, :, :, 1].transpose(1, 2, 0, 3).reshape(4, UNIT)
    return jnp.stack([low, high])


def in_query_order(units):
    low = units[:4].reshape(4, 4, 8, PER).transpose(2, 1, 0, 3)
    high = units[4:].reshape(4, 4, 8, PER).transpose(2, 0, 1, 3)
    return jnp.stack([low, high], axis=3).reshape(-1)


def on_device(queries, candidates, targets):
    z, u, v, c = place()
    owner = z * 32 + lax.axis_index("shard")
    t = in_place_order(targets - owner * candidates.shape[0])
    slots = [None] * 8
    for far in range(4):
        slots[OWN[far]] = t[c, (u + far) % 4]
        slots[OTHER[far]] = t[1 - c, (v + far) % 4]
    every = gather(queries)
    partial = score(every, candidates, jnp.concatenate(slots)[None])
    out = reduced(partial)
    units = jnp.concatenate([out[:, 0], out[:, 1, 64:]], axis=1)
    losses = in_query_order(units)
    return losses, jnp.mean(losses)


def solution(mesh):
    whole = P(("group", "shard"), None)
    return jax.shard_map(
        on_device, mesh=mesh, in_specs=(whole, whole, P()), out_specs=(P(), P()), check_vma=False
    )
```

time: 196 us -> 85.6 us (0.44)
  Pallas kernels: 0 us -> 74.5 us
  blocking collectives: 71.9 us -> 0 us
  waiting for transfers between devices: 40.6 us -> 0 us
  local copies, waits for them, and re-layouts: 31.7 us -> 5.9 us
  matrix products: 21.4 us -> 0 us
  between operations: 16.2 us -> 3.42 us
  other arithmetic: 13.4 us -> 1.32 us
    pallas_call x0 -> x3, Pallas kernels: none -> 74.5 us  [the longest x1 35.3 us: gather(): pl.pallas_call(gather_kernel, out_shape=jax.ShapeDtypeStruct((8 * UNIT, q...]
    all_gather x2 -> x0, waiting for transfers between devices: 40.6 us -> none  [gather_in_order(): tiles = lax.all_gather(tiles, axes[k], axis=0, tiled=True)]
    all_to_all x2 -> x0, blocking collectives: 38.3 us -> none  [from_everyone(): return lax.all_to_all(copies, axis, split_axis=0, concat_axis=0, tiled=True)]
    all_gather x2 -> x0, blocking collectives: 33.7 us -> none  [gather_in_order(): tiles = lax.all_gather(tiles, axes[k], axis=0, tiled=True)]
    dot_general x3 -> x0, matrix products: 21.4 us -> none  [score_panel(): scores = jnp.dot(panel, candidates.T, preferred_element_type=jnp.float32)]
    gather x2 -> x0, local copies, waits for them, and re-layouts: 14.5 us -> none  [score_rows(): chosen = jnp.take(candidates, jnp.clip(local, 0, rows - 1), axis=0)]
    reduce_sum x4 -> x0, other arithmetic: 11.6 us -> none  [the longest x1 7.8 us: score_rows(): jnp.sum(piece.astype(jnp.float32) * chosen.astype(jnp.float32), axis=1)]
    another operation x1 -> x4, local copies, waits for them, and re-layouts: 4.87 us -> 0.32 us  [the longest x3 0.22 us: in_place_order(): return jnp.stack([low, high])]
  transfers between devices with their start and end apart: 2 -> 0, of which waited for: 2 -> 0; matrix products, arithmetic and copies ran while one was open for 8% -> 0% of each run, Pallas kernels for 0% -> 0%
where the time goes in v1:
time: 85.6 us; the launch traced here: 85.2 us
  Pallas kernels  74.5 us (87%)
  local copies, waits for them, and re-layouts  5.9 us (7%)
  between operations  3.42 us (4%)
  other arithmetic  1.32 us (2%)
    pallas_call x1, Pallas kernels, gather(): pl.pallas_call(gather_kernel, out_shape=jax.ShapeDtypeStruct((8 * UNIT, q...  35.3 us
    pallas_call x1, Pallas kernels, score(): pl.pallas_call(functools.partial(score_kernel, rows, cols), out_shape=jax...  19.7 us
    pallas_call x1, Pallas kernels, reduced(): pl.pallas_call(reduce_kernel, out_shape=jax.ShapeDtypeStruct((8, *tile),...  19.5 us
    unnamed x5, local copies, waits for them, and re-layouts  2.48 us

profile of v1, /device:TPU:1, one launch (start us, length us, event | category | flops | bytes accessed | tf_op | source)
XLA Modules:
  0.0 85.2 jit_solution(5756843752390903225)
XLA Ops:
  0.8 0.7 broadcast_subtract_fusion
  1.6 0.2 reshape.16
  1.8 0.1 fusion.4
  1.9 0.1 stack_reshape.7
  2.1 0.1 stack_reshape.6
  2.2 0.1 concatenate.6
  2.3 35.3 %gather_queries.1.q_ref = bf16[1536,1024]{1,0:T(8,128)(2,1)} custom-call(bf16[6,1024]{1,0:T(8,128)(2,1)} %q_ref.1), custom_call_target="tpu_custom_call" | custom-call | tf_op jit(solution)/shard_map/gather_queries/pallas_call | solution.py:113
  37.7 0.0 copy-start
  37.7 1.9 %copy-done = bf16[1536,1024]{1,0:T(8,128)(2,1)S(1)} copy-done((bf16[1536,1024]{1,0:T(8,128)(2,1)S(1)}, bf16[1536,1024]{1,0:T(8,128)(2,1)}, u32[]{:S(2)}) %copy-start) | copy-done | bytes 3145752
  39.6 19.7 %score_queries.1.r_ref = f32[8,8,128]{2,1,0:T(8,128)S(1)} custom-call(bf16[1536,1024]{1,0:T(8,128)(2,1)S(1)} %copy-done, bf16[4096,1024]{1,0:T(8,128)(2,1)} %c_hbm.1, s32[1,1536]{1,0:T(1,128)S(1)} %broadcast_in_dim.3.t_ref), custom_call_target="tpu_custom_call" | custom-call | tf_op jit(solution)/shard_map/score_queries/pallas_call | solution.py:199
  59.3 0.0 copy-start.1
  59.3 0.6 copy-done.1
  59.9 19.5 %reduce_losses.1 = f32[8,8,128]{2,1,0:T(8,128)} custom-call(f32[8,8,128]{2,1,0:T(8,128)} %copy-done.1), custom_call_target="tpu_custom_call" | custom-call | tf_op jit(solution)/shard_map/reduce_losses/pallas_call | solution.py:294
  79.4 0.8 slice.21
  80.2 0.8 slice.20
  81.0 0.6 fusion.2
  82.9 0.1 reshape.17
  83.0 0.1 reshape.18
  83.1 0.1 copy.9
  83.2 0.8 reshape.19
  (8 shorter events, 0.1 us)
Async XLA Ops:
  37.7 1.9 %copy-start = (bf16[1536,1024]{1,0:T(8,128)(2,1)S(1)}, bf16[1536,1024]{1,0:T(8,128)(2,1)}, u32[]{:S(2)}) copy-start(bf16[1536,1024]{1,0:T(8,128)(2,1)} %gather_queries.1.q_ref) | copy-start | bytes 9437188
  59.3 0.6 copy-start.1

commit v2 on v0

v2 whole, which is shorter than its diff:
```python
import functools

import jax
import jax.numpy as jnp
from jax import lax
from jax.experimental import pallas as pl
from jax.experimental.pallas import tpu as pltpu
from jax.sharding import PartitionSpec as P

F32 = jnp.float32
BF16 = jnp.bfloat16
MESH = pl.DeviceIdType.MESH
LOW = -3.0e38
PER = 6
BLOCK = 48
UNIT = 192
OWN = {0: 0, 1: 2, 3: 3, 2: 6}
OTHER = {0: 1, 1: 4, 3: 5, 2: 7}
NEAR_FIRST = (1, 3, 2)
BATCHES = ((0, 256), (256, 512), (768, 512), (1280, 256))


def place():
    z = lax.axis_index("group")
    s = lax.axis_index("shard")
    x, y, c = s // 8, (s // 2) % 4, s % 2
    u = y * (1 - c) + x * c
    v = x * (1 - c) + y * c
    return z, u, v, c


def at(z, u, v, c):
    x = v * (1 - c) + u * c
    y = u * (1 - c) + v * c
    return (z, (x * 4 + y) * 2 + c)


def rows_of(slot, v):
    return pl.ds(pl.multiple_of(slot * UNIT + v * BLOCK, 16), BLOCK)


def meet(others):
    barrier = pltpu.get_barrier_semaphore()
    for other in others:
        pl.semaphore_signal(barrier, inc=1, device_id=other, device_id_type=MESH)
    pl.semaphore_wait(barrier, len(others))


def scored_batch(c_buf, q_ref, t_ref, first, cols, s0, s1):
    rows = s0.shape[0]
    blocks = c_buf.shape[0] // rows
    groups = rows // 8
    q_rows = pl.ds(first, cols)
    wanted = jnp.broadcast_to(t_ref[:, first : first + cols], (8, cols))
    wanted = wanted - lax.broadcasted_iota(jnp.int32, (8, cols), 0)

    def scored(k, held):
        part = c_buf[pl.ds(pl.multiple_of(k * rows, rows), rows), :]
        scores = lax.dot_general(part, q_ref[q_rows, :], (((1,), (1,)), ((), ())), preferred_element_type=F32)
        held[...] = scores
        return scores

    def peak(scores, top):
        return jnp.maximum(top, jnp.max(scores.reshape(groups, 8, cols), axis=0))

    def take(held, k, old, new, total, picked):
        total = total * jnp.exp(old - new)
        for g in range(groups):
            value = held[g * 8 : (g + 1) * 8, :]
            total = total + jnp.exp(value - new)
            picked = jnp.where(wanted == k * rows + g * 8, value, picked)
        return total, picked

    def step(j, carry):
        old, new, total, picked = carry
        newer = peak(scored(2 * j + 1, s1), new)
        total, picked = take(s0, 2 * j, old, new, total, picked)
        newest = peak(scored(2 * j + 2, s0), newer)
        total, picked = take(s1, 2 * j + 1, new, newer, total, picked)
        return newer, newest, total, picked

    old = jnp.full((8, cols), LOW, F32)
    zero = jnp.zeros((8, cols), F32)
    carry = (old, peak(scored(0, s0), old), zero, zero)
    old, new, total, picked = lax.fori_loop(0, blocks // 2 - 1, step, carry)
    newer = peak(scored(blocks - 1, s1), new)
    total, picked = take(s0, blocks - 2, old, new, total, picked)
    total, picked = take(s1, blocks - 1, new, newer, total, picked)
    top = jnp.max(newer, axis=0, keepdims=True)
    total = jnp.sum(total * jnp.exp(newer - top), axis=0, keepdims=True)
    return top, total, jnp.sum(picked, axis=0, keepdims=True)


def loss_kernel(
    q_ref, c_hbm, t_ref, o_ref,
    c_buf, all_ref, first, narrow0, narrow1, wide0, wide1,
    partial, from_core, at_x, from_x, at_y, from_y, at_z, from_z, mine,
    loaded, send1, recv1, send2, recv2, send3, recv3, sendp, recvp, sends, recvs,
):
    z, u, v, c = place()
    x = v * (1 - c) + u * c
    y = u * (1 - c) + v * c

    def device(z, x, y, c):
        return (z, (x * 4 + y) * 2 + c)

    chunk = c_buf.shape[0] // loaded.shape[0]
    loads = [
        pltpu.make_async_copy(c_hbm.at[pl.ds(i * chunk, chunk)], c_buf.at[pl.ds(i * chunk, chunk)], loaded.at[i])
        for i in range(loaded.shape[0])
    ]
    for load in loads:
        load.start()
    partner = device(z, x, y, 1 - c)
    column = [device((z + d) % 8, x, y, c) for d in range(1, 8)]
    xs = [device(z, (x + d) % 4, y, c) for d in range(1, 4)]
    ys = [device(z, x, (y + d) % 4, c) for d in range(1, 4)]
    crossed = [device(z, (x + d) % 4, y, 1 - c) for d in range(1, 4)]
    along_v = {d: at(z, u, (v + d) % 4, c) for d in NEAR_FIRST}
    along_u = {d: at(z, (u + d) % 4, v, c) for d in NEAR_FIRST}
    meet(column + xs + ys + crossed + [partner])
    sent = []

    def copy(src, dst, send, recv, to):
        return pltpu.make_async_remote_copy(
            src_ref=src, dst_ref=dst, send_sem=send, recv_sem=recv, device_id=to, device_id_type=MESH
        )

    def start(*args):
        one = copy(*args)
        one.start()
        sent.append(one)

    first[z] = q_ref[...]
    for d in (4, 3, 5, 2, 6, 1, 7):
        start(q_ref, first.at[z], send1.at[d], recv1.at[d], column[d - 1])
    for d in (1, 7, 2, 6, 3, 5, 4):
        here = first.at[(z + 8 - d) % 8]
        copy(here, here, send1.at[d], recv1.at[d], column[d - 1]).wait_recv()
    block = jnp.concatenate([first[k].astype(F32) for k in range(8)], axis=0)
    all_ref[rows_of(0, v), :] = block.astype(BF16)

    def to_partner(far, d):
        held = all_ref.at[rows_of(OWN[far], (v + 4 - d) % 4)]
        there = all_ref.at[rows_of(OTHER[far], (v + 4 - d) % 4)]
        start(held, there, sendp.at[far, d], recvp.at[far, d], partner)

    def along(e, d):
        held = all_ref.at[rows_of(0, (v + 4 - d) % 4)]
        there = all_ref.at[rows_of(OWN[(4 - e) % 4], (v + 4 - d) % 4)]
        start(held, there, send3.at[e, d], recv3.at[e, d], along_u[e])

    def arrived_along(e, d):
        here = all_ref.at[rows_of(OWN[(4 - e) % 4], (v + 4 - d) % 4)]
        copy(here, here, send3.at[e, d], recv3.at[e, d], along_u[e]).wait_recv()

    def from_partner(far):
        for d in range(4):
            here = all_ref.at[rows_of(OTHER[far], (u + 4 - d) % 4)]
            copy(here, here, sendp.at[far, d], recvp.at[far, d], partner).wait_recv()

    own = all_ref.at[rows_of(0, v)]
    for d in NEAR_FIRST:
        start(own, own, send2.at[d], recv2.at[d], along_v[d])
    to_partner(0, 0)
    along(1, 0)
    along(3, 0)
    for d in NEAR_FIRST:
        here = all_ref.at[rows_of(0, (v + 4 - d) % 4)]
        copy(here, here, send2.at[d], recv2.at[d], along_v[d]).wait_recv()
        to_partner(0, d)
        along(1, d)
        along(3, d)
    for d in (0, 1, 3, 2):
        along(2, d)
    for load in loads:
        load.wait()
    from_partner(0)

    results = []

    def run(k):
        begin, cols = BATCHES[k]
        held = (narrow0, narrow1) if cols == narrow0.shape[1] else (wide0, wide1)
        results.append(scored_batch(c_buf, all_ref, t_ref, begin, cols, *held))

    run(0)
    for d in (0, 1, 3, 2):
        for e in (1, 3):
            arrived_along(e, d)
            to_partner((4 - e) % 4, d)
    run(1)
    for d in (0, 1, 3, 2):
        arrived_along(2, d)
        to_partner(2, d)
    from_partner(1)
    from_partner(3)
    run(2)
    from_partner(2)
    run(3)

    lines = [jnp.concatenate(parts, axis=1) for parts in zip(*results)]
    for far in range(4):
        for slot, unit in ((OWN[far], c * 4 + (u + far) % 4), (OTHER[far], (1 - c) * 4 + (v + far) % 4)):
            parts = []
            for line in lines:
                parts.append(line[:, slot * UNIT : slot * UNIT + 128])
                parts.append(line[:, slot * UNIT + 64 : slot * UNIT + 192])
            partial[unit] = jnp.concatenate(parts + [jnp.zeros((2, 128), F32)], axis=0)

    def pass_on(k, src, dst, to):
        start(src, dst, sends.at[k], recvs.at[k], to)

    def wait(k, here):
        copy(here, here, sends.at[k], recvs.at[k], partner).wait_recv()

    pass_on(0, partial.at[pl.ds((1 - c) * 4, 4)], from_core, partner)
    wait(0, from_core)
    for k in range(4):
        at_x[k] = combined([partial[c * 4 + k], from_core[k]])
    for d in range(1, 4):
        pass_on(d, at_x.at[(x + d) % 4], from_x.at[d], xs[d - 1])
    for d in range(1, 4):
        wait(d, from_x.at[d])
    at_y[...] = combined([at_x[x]] + [from_x[d] for d in range(1, 4)])
    for d in range(1, 4):
        pass_on(3 + d, at_y, from_y.at[d], ys[d - 1])
    for d in range(1, 4):
        wait(3 + d, from_y.at[d])
    at_z[...] = combined([at_y[...]] + [from_y[d] for d in range(1, 4)])
    for d in (4, 3, 5, 2, 6, 1, 7):
        pass_on(6 + d, at_z, from_z.at[d], column[d - 1])
    for d in range(1, 8):
        wait(6 + d, from_z.at[d])
    whole = combined([at_z[...]] + [from_z[d] for d in range(1, 8)])
    loss = whole[0:2] + jnp.log(whole[2:4]) - whole[4:6]
    mine[...] = jnp.concatenate([loss, jnp.zeros((6, 128), F32)], axis=0)
    unit = c * 4 + x
    o_ref[unit] = mine[...]
    for d in range(7):
        pass_on(14 + d, mine, o_ref.at[unit], ([partner] + xs + crossed)[d])
    for d in range(7):
        colour = c * 4 if 1 <= d < 4 else (1 - c) * 4
        wait(14 + d, o_ref.at[colour + (x + 4 - (0, 1, 2, 3, 1, 2, 3)[d]) % 4])
    for one in sent:
        one.wait_send()


def all_losses(queries, candidates, targets):
    count, width = candidates.shape
    tile = (8, 128)
    dma = pltpu.SemaphoreType.DMA
    return pl.pallas_call(
        loss_kernel,
        out_shape=jax.ShapeDtypeStruct((8, *tile), F32),
        in_specs=[
            pl.BlockSpec(memory_space=pltpu.VMEM),
            pl.BlockSpec(memory_space=pl.ANY),
            pl.BlockSpec(memory_space=pltpu.VMEM),
        ],
        out_specs=pl.BlockSpec(memory_space=pltpu.VMEM),
        scratch_shapes=[
            pltpu.VMEM((count, width), BF16),
            pltpu.VMEM((8 * UNIT, width), BF16),
            pltpu.VMEM((8, PER, width), BF16),
            pltpu.VMEM((1024, 256), F32),
            pltpu.VMEM((1024, 256), F32),
            pltpu.VMEM((512, 512), F32),
            pltpu.VMEM((512, 512), F32),
            pltpu.VMEM((8, *tile), F32),
            pltpu.VMEM((4, *tile), F32),
            pltpu.VMEM((4, *tile), F32),
            pltpu.VMEM((4, *tile), F32),
            pltpu.VMEM(tile, F32),
            pltpu.VMEM((4, *tile), F32),
            pltpu.VMEM(tile, F32),
            pltpu.VMEM((8, *tile), F32),
            pltpu.VMEM(tile, F32),
        ]
        + [dma((4,)), dma((8,)), dma((8,)), dma((4,)), dma((4,)), dma((4, 4)), dma((4, 4)), dma((4, 4)), dma((4, 4))]
        + [dma((21,)), dma((21,))],
        compiler_params=pltpu.CompilerParams(
            collective_id=1, has_side_effects=True, vmem_limit_bytes=50 << 20
        ),
        name="ranking_losses",
    )(queries, candidates, targets)


def combined(tiles):
    tops = [tile[0:2] for tile in tiles]
    top = functools.reduce(jnp.maximum, tops)
    total = sum(tile[2:4] * jnp.exp(one - top) for tile, one in zip(tiles, tops))
    picked = sum(tile[4:6] for tile in tiles)
    return jnp.concatenate([top, total, picked, jnp.zeros((2, 128), F32)], axis=0)


def in_place_order(targets):
    t = targets.reshape(8, 4, 4, 2, PER)
    low = t[:, :, :, 0].transpose(2, 1, 0, 3).reshape(4, UNIT)
    high = t[:, :, :, 1].transpose(1, 2, 0, 3).reshape(4, UNIT)
    return jnp.stack([low, high])


def in_query_order(units):
    low = units[:4].reshape(4, 4, 8, PER).transpose(2, 1, 0, 3)
    high = units[4:].reshape(4, 4, 8, PER).transpose(2, 0, 1, 3)
    return jnp.stack([low, high], axis=3).reshape(-1)


def on_device(queries, candidates, targets):
    z, u, v, c = place()
    owner = z * 32 + lax.axis_index("shard")
    t = in_place_order(targets - owner * candidates.shape[0])
    slots = [None] * 8
    for far in range(4):
        slots[OWN[far]] = t[c, (u + far) % 4]
        slots[OTHER[far]] = t[1 - c, (v + far) % 4]
    out = all_losses(queries, candidates, jnp.concatenate(slots)[None])
    units = jnp.concatenate([out[:, 0], out[:, 1, 64:]], axis=1)
    losses = in_query_order(units)
    return losses, jnp.mean(losses)


def solution(mesh):
    whole = P(("group", "shard"), None)
    return jax.shard_map(
        on_device, mesh=mesh, in_specs=(whole, whole, P()), out_specs=(P(), P()), check_vma=False
    )
```

time: 196 us -> 69 us (0.35)
  blocking collectives: 71.9 us -> 0 us
  Pallas kernels: 0 us -> 61.2 us
  waiting for transfers between devices: 40.6 us -> 0 us
  local copies, waits for them, and re-layouts: 31.7 us -> 2.62 us
  matrix products: 21.4 us -> 0 us
  between operations: 16.2 us -> 3.43 us
  other arithmetic: 13.4 us -> 1.41 us
    pallas_call x0 -> x1, Pallas kernels: none -> 61.2 us  [all_losses(): pl.pallas_call(loss_kernel, out_shape=jax.ShapeDtypeStruct((8, *tile), F3...]
    all_gather x2 -> x0, waiting for transfers between devices: 40.6 us -> none  [gather_in_order(): tiles = lax.all_gather(tiles, axes[k], axis=0, tiled=True)]
    all_to_all x2 -> x0, blocking collectives: 38.3 us -> none  [from_everyone(): return lax.all_to_all(copies, axis, split_axis=0, concat_axis=0, tiled=True)]
    all_gather x2 -> x0, blocking collectives: 33.7 us -> none  [gather_in_order(): tiles = lax.all_gather(tiles, axes[k], axis=0, tiled=True)]
    dot_general x3 -> x0, matrix products: 21.4 us -> none  [score_panel(): scores = jnp.dot(panel, candidates.T, preferred_element_type=jnp.float32)]
    gather x2 -> x0, local copies, waits for them, and re-layouts: 14.5 us -> none  [score_rows(): chosen = jnp.take(candidates, jnp.clip(local, 0, rows - 1), axis=0)]
    reduce_sum x4 -> x0, other arithmetic: 11.6 us -> none  [the longest x1 7.8 us: score_rows(): jnp.sum(piece.astype(jnp.float32) * chosen.astype(jnp.float32), axis=1)]
    another operation x1 -> x4, local copies, waits for them, and re-layouts: 4.87 us -> 0.32 us  [the longest x3 0.22 us: in_place_order(): return jnp.stack([low, high])]
  transfers between devices with their start and end apart: 2 -> 0, of which waited for: 2 -> 0; matrix products, arithmetic and copies ran while one was open for 8% -> 0% of each run, Pallas kernels for 0% -> 0%
where the time goes in v2:
time: 69 us; the launch traced here: 68.7 us
  Pallas kernels  61.2 us (89%)
  between operations  3.43 us (5%)
  local copies, waits for them, and re-layouts  2.62 us (4%)
  other arithmetic  1.41 us (2%)
    pallas_call x1, Pallas kernels, all_losses(): pl.pallas_call(loss_kernel, out_shape=jax.ShapeDtypeStruct((8, *tile), F3...  61.2 us

profile of v2, /device:TPU:1, one launch (start us, length us, event | category | flops | bytes accessed | tf_op | source)
XLA Modules:
  0.0 68.7 jit_solution(11009028692921854102)
XLA Ops:
  0.6 0.7 %broadcast_subtract_fusion = s32[1536]{0:T(1024)S(1)} fusion(s32[1536]{0:T(1024)} %param.5, s32[]{:T(128)S(6)} %mul.19), kind=kLoop, calls=%fused_computation.8 | loop fusion | flops 1536 | bytes 12292 | tf_op jit(solution)/shard_map/sub | solution.py:313
  1.3 0.2 reshape.16
  1.6 0.1 fusion.4
  1.7 0.1 stack_reshape.6
  1.9 0.1 stack_reshape.7
  2.2 0.1 concatenate.6
  2.3 0.0 copy-start
  2.3 0.7 %copy-done = bf16[6,1024]{1,0:T(8,128)(2,1)S(1)} copy-done((bf16[6,1024]{1,0:T(8,128)(2,1)S(1)}, bf16[6,1024]{1,0:T(8,128)(2,1)}, u32[]{:S(2)}) %copy-start) | copy-done | bytes 12312
  3.0 61.2 %ranking_losses.1 = f32[8,8,128]{2,1,0:T(8,128)S(1)} custom-call(bf16[6,1024]{1,0:T(8,128)(2,1)S(1)} %copy-done, bf16[4096,1024]{1,0:T(8,128)(2,1)} %c_hbm.1, s32[1,1536]{1,0:T(1,128)S(1)} %broadcast_in_dim.3.t_ref), custom_call_target="tpu_custom_call" | custom-call | tf_op jit(solution)/shard_map/ranking_losses/pallas_call | solution.py:253
  64.3 0.1 slice.21
  64.4 0.7 %fusion.2 = (f32[]{:T(128)}, f32[4,192]{1,0:T(4,128)S(1)}, f32[]{:T(128)}, f32[4,192]{1,0:T(4,128)S(1)}) fusion(f32[8,64]{1,0:T(8,128)S(1)} %bitcast.32, f32[8,128]{1,0:T(8,128)S(1)} %bitcast.33), kind=kLoop, calls=%fused_computation.18 | loop fusion | flops 3070 | bytes 12296 | tf_op jit(solution)/shard_map/reduce_sum | solution.py:321
  65.1 0.1 reshape.18
  65.2 0.1 reshape.17
  65.3 0.1 copy.9
  65.4 0.8 %reshape.19 = f32[1536]{0:T(1024)} reshape(f32[8,4,4,2,6]{4,3,2,1,0:T(2,128)S(1)} %copy.9) | data formatting | bytes 12288 | tf_op jit(solution)/shard_map/reshape | solution.py:307
  (9 shorter events, 0.1 us)
Async XLA Ops:
  2.3 0.7 %copy-start = (bf16[6,1024]{1,0:T(8,128)(2,1)S(1)}, bf16[6,1024]{1,0:T(8,128)(2,1)}, u32[]{:S(2)}) copy-start(bf16[6,1024]{1,0:T(8,128)(2,1)} %q_ref.1) | copy-start | bytes 36868

commit v3 on v2

--- a/solution.py
+++ b/solution.py
@@ -17,6 +17,7 @@
 OWN = {0: 0, 1: 2, 3: 3, 2: 6}
 OTHER = {0: 1, 1: 4, 3: 5, 2: 7}
 NEAR_FIRST = (1, 3, 2)
+RELAYED_BY = (1, 3, 1, 3)
 BATCHES = ((0, 256), (256, 512), (768, 512), (1280, 256))
 
 
@@ -44,6 +45,56 @@
     for other in others:
         pl.semaphore_signal(barrier, inc=1, device_id=other, device_id_type=MESH)
     pl.semaphore_wait(barrier, len(others))
+
+
+def flat_place(l, colour, u):
+    v = (l * 1366) >> 16
+    l = l - v * BLOCK
+    z = (l * 10923) >> 16
+    r = l - z * PER
+    chip = v * (4 - 3 * colour) + u * (1 + 3 * colour)
+    return z * UNIT + chip * 2 * PER + colour * PER + r
+
+
+def exact_parts(a):
+    high = a.astype(BF16)
+    rest = a - high.astype(F32)
+    middle = rest.astype(BF16)
+    return high, middle, (rest - middle.astype(F32)).astype(BF16)
+
+
+def own_targets(targets, owner, rows, slots):
+    local = targets - owner * rows
+    local = jnp.where((local >= 0) & (local < rows), local, rows)
+    pad = jnp.zeros((4, 128), jnp.int32)
+    both = jnp.concatenate([local >> 6, pad, local & 63, pad], axis=0).astype(F32).astype(BF16)
+    lines = []
+    for colour, u in slots:
+        flat = flat_place(lax.broadcasted_iota(jnp.int32, (1, UNIT), 1), colour, u)
+        lane = lax.broadcasted_iota(jnp.int32, (128, UNIT), 0) == (flat & 127)
+        found = jnp.dot(both, jnp.where(lane, 1.0, 0.0).astype(BF16), preferred_element_type=F32)
+        row = lax.broadcasted_iota(jnp.int32, (16, UNIT), 0) == (flat >> 7)
+        value = jnp.where(row, found[0:16] * 64.0 + found[16:32], 0.0)
+        lines.append(jnp.sum(value, axis=0, keepdims=True))
+    return jnp.concatenate(lines, axis=1).astype(jnp.int32)
+
+
+def selector(colour, u, half):
+    flat = flat_place(lax.broadcasted_iota(jnp.int32, (128, 128), 0) + half * 64, colour, u)
+    lane = lax.broadcasted_iota(jnp.int32, (128, 128), 1) == (flat & 127)
+    return jnp.where(lane, 1.0, 0.0).astype(BF16)
+
+
+def in_order(loss, select, colour, u):
+    total = None
+    for half in range(2):
+        l = lax.broadcasted_iota(jnp.int32, (16, 128), 1) + half * 64
+        here = lax.broadcasted_iota(jnp.int32, (16, 128), 0) == (flat_place(l, colour, u) >> 7)
+        here = here & (l >= half * 128)
+        parts = [jnp.where(here, part.astype(F32), 0.0).astype(BF16) for part in exact_parts(loss[half : half + 1])]
+        found = jnp.dot(jnp.concatenate(parts, axis=0), select[half], preferred_element_type=F32)
+        total = found if total is None else total + found
+    return (total[0:16] + total[16:32]) + total[32:48]
 
 
 def scored_batch(c_buf, q_ref, t_ref, first, cols, s0, s1):
@@ -92,10 +143,10 @@
 
 
 def loss_kernel(
-    q_ref, c_hbm, t_ref, o_ref,
-    c_buf, all_ref, first, narrow0, narrow1, wide0, wide1,
-    partial, from_core, at_x, from_x, at_y, from_y, at_z, from_z, mine,
-    loaded, send1, recv1, send2, recv2, send3, recv3, sendp, recvp, sends, recvs,
+    q_hbm, c_hbm, t_hbm, o_ref, mean_ref,
+    t_nat, t_ref, select, c_buf, all_ref, first, narrow0, narrow1, wide0, wide1,
+    partial, from_row, at_y, from_y, at_z, from_z, shared,
+    small, loaded, send1, recv1, send2, recv2, send3, recv3, sendp, recvp, sends, recvs,
 ):
     z, u, v, c = place()
     x = v * (1 - c) + u * c
@@ -109,8 +160,10 @@
         pltpu.make_async_copy(c_hbm.at[pl.ds(i * chunk, chunk)], c_buf.at[pl.ds(i * chunk, chunk)], loaded.at[i])
         for i in range(loaded.shape[0])
     ]
-    for load in loads:
-        load.start()
+    ask = pltpu.make_async_copy(q_hbm, first.at[z], small.at[0])
+    ask_t = pltpu.make_async_copy(t_hbm, t_nat, small.at[1])
+    ask.start()
+    ask_t.start()
     partner = device(z, x, y, 1 - c)
     column = [device((z + d) % 8, x, y, c) for d in range(1, 8)]
     xs = [device(z, (x + d) % 4, y, c) for d in range(1, 4)]
@@ -119,6 +172,9 @@
     along_v = {d: at(z, u, (v + d) % 4, c) for d in NEAR_FIRST}
     along_u = {d: at(z, (u + d) % 4, v, c) for d in NEAR_FIRST}
     meet(column + xs + ys + crossed + [partner])
+    for load in loads:
+        load.start()
+    ask.wait()
     sent = []
 
     def copy(src, dst, send, recv, to):
@@ -131,9 +187,17 @@
         one.start()
         sent.append(one)
 
-    first[z] = q_ref[...]
     for d in (4, 3, 5, 2, 6, 1, 7):
-        start(q_ref, first.at[z], send1.at[d], recv1.at[d], column[d - 1])
+        start(first.at[z], first.at[z], send1.at[d], recv1.at[d], column[d - 1])
+    slots = [None] * 8
+    for far in range(4):
+        slots[OWN[far]] = c, (u + far) % 4
+        slots[OTHER[far]] = 1 - c, (v + far) % 4
+    ask_t.wait()
+    owner = z * 32 + lax.axis_index("shard")
+    t_ref[...] = own_targets(t_nat[...], owner, c_buf.shape[0], slots)
+    for half in range(2):
+        select[half] = selector(c, x, half)
     for d in (1, 7, 2, 6, 3, 5, 4):
         here = first.at[(z + 8 - d) % 8]
         copy(here, here, send1.at[d], recv1.at[d], column[d - 1]).wait_recv()
@@ -160,7 +224,7 @@
             copy(here, here, sendp.at[far, d], recvp.at[far, d], partner).wait_recv()
 
     own = all_ref.at[rows_of(0, v)]
-    for d in NEAR_FIRST:
+    for d in (2, 1, 3):
         start(own, own, send2.at[d], recv2.at[d], along_v[d])
     to_partner(0, 0)
     along(1, 0)
@@ -171,8 +235,6 @@
         to_partner(0, d)
         along(1, d)
         along(3, d)
-    for d in (0, 1, 3, 2):
-        along(2, d)
     for load in loads:
         load.wait()
     from_partner(0)
@@ -188,6 +250,10 @@
     for d in (0, 1, 3, 2):
         for e in (1, 3):
             arrived_along(e, d)
+            if e == RELAYED_BY[d]:
+                held = all_ref.at[rows_of(OWN[(4 - e) % 4], (v + 4 - d) % 4)]
+                there = all_ref.at[rows_of(OWN[2], (v + 4 - d) % 4)]
+                start(held, there, send3.at[2, d], recv3.at[2, d], along_u[e])
             to_partner((4 - e) % 4, d)
     run(1)
     for d in (0, 1, 3, 2):
@@ -200,13 +266,12 @@
     run(3)
 
     lines = [jnp.concatenate(parts, axis=1) for parts in zip(*results)]
-    for far in range(4):
-        for slot, unit in ((OWN[far], c * 4 + (u + far) % 4), (OTHER[far], (1 - c) * 4 + (v + far) % 4)):
-            parts = []
-            for line in lines:
-                parts.append(line[:, slot * UNIT : slot * UNIT + 128])
-                parts.append(line[:, slot * UNIT + 64 : slot * UNIT + 192])
-            partial[unit] = jnp.concatenate(parts + [jnp.zeros((2, 128), F32)], axis=0)
+    for slot, (colour, there) in enumerate(slots):
+        parts = []
+        for line in lines:
+            parts.append(line[:, slot * UNIT : slot * UNIT + 128])
+            parts.append(line[:, slot * UNIT + 64 : slot * UNIT + 192])
+        partial[colour * 4 + there] = jnp.concatenate(parts + [jnp.zeros((2, 128), F32)], axis=0)
 
     def pass_on(k, src, dst, to):
         start(src, dst, sends.at[k], recvs.at[k], to)
@@ -214,15 +279,14 @@
     def wait(k, here):
         copy(here, here, sends.at[k], recvs.at[k], partner).wait_recv()
 
-    pass_on(0, partial.at[pl.ds((1 - c) * 4, 4)], from_core, partner)
-    wait(0, from_core)
-    for k in range(4):
-        at_x[k] = combined([partial[c * 4 + k], from_core[k]])
-    for d in range(1, 4):
-        pass_on(d, at_x.at[(x + d) % 4], from_x.at[d], xs[d - 1])
-    for d in range(1, 4):
-        wait(d, from_x.at[d])
-    at_y[...] = combined([at_x[x]] + [from_x[d] for d in range(1, 4)])
+    unit = c * 4 + x
+    row = [None] + [((x + k // 2) % 4, (c + k) % 2) for k in range(1, 8)]
+    for k in (4, 5, 2, 3, 6, 7, 1):
+        there, core = row[k]
+        pass_on(13 + k, partial.at[core * 4 + there], from_row.at[k], device(z, there, y, core))
+    for k in range(1, 8):
+        wait(13 + k, from_row.at[k])
+    at_y[...] = combined([partial[unit]] + [from_row[k] for k in range(1, 8)])
     for d in range(1, 4):
         pass_on(3 + d, at_y, from_y.at[d], ys[d - 1])
     for d in range(1, 4):
@@ -234,14 +298,15 @@
         wait(6 + d, from_z.at[d])
     whole = combined([at_z[...]] + [from_z[d] for d in range(1, 8)])
     loss = whole[0:2] + jnp.log(whole[2:4]) - whole[4:6]
-    mine[...] = jnp.concatenate([loss, jnp.zeros((6, 128), F32)], axis=0)
-    unit = c * 4 + x
-    o_ref[unit] = mine[...]
-    for d in range(7):
-        pass_on(14 + d, mine, o_ref.at[unit], ([partner] + xs + crossed)[d])
-    for d in range(7):
-        colour = c * 4 if 1 <= d < 4 else (1 - c) * 4
-        wait(14 + d, o_ref.at[colour + (x + 4 - (0, 1, 2, 3, 1, 2, 3)[d]) % 4])
+    shared[0] = in_order(loss, select, c, x)
+    for k in (4, 5, 2, 3, 6, 7, 1):
+        there, core = row[k]
+        pass_on(20 + k, shared.at[0], shared.at[k], device(z, there, y, core))
+    for k in range(1, 8):
+        wait(20 + k, shared.at[k])
+    every = ((shared[0] + shared[1]) + (shared[2] + shared[3])) + ((shared[4] + shared[5]) + (shared[6] + shared[7]))
+    o_ref[...] = every[0:12]
+    mean_ref[...] = jnp.sum(every, keepdims=True) * (1.0 / (8 * UNIT))
     for one in sent:
         one.wait_send()
 
@@ -252,14 +317,17 @@
     dma = pltpu.SemaphoreType.DMA
     return pl.pallas_call(
         loss_kernel,
-        out_shape=jax.ShapeDtypeStruct((8, *tile), F32),
+        out_shape=(jax.ShapeDtypeStruct((12, 128), F32), jax.ShapeDtypeStruct((1, 1), F32)),
         in_specs=[
-            pl.BlockSpec(memory_space=pltpu.VMEM),
-            pl.BlockSpec(memory_space=pl.ANY),
-            pl.BlockSpec(memory_space=pltpu.VMEM),
+            pl.BlockSpec(memory_space=pltpu.HBM),
+            pl.BlockSpec(memory_space=pltpu.HBM),
+            pl.BlockSpec(memory_space=pltpu.HBM),
         ],
-        out_specs=pl.BlockSpec(memory_space=pltpu.VMEM),
+        out_specs=(pl.BlockSpec(memory_space=pltpu.VMEM), pl.BlockSpec(memory_space=pltpu.VMEM)),
         scratch_shapes=[
+            pltpu.VMEM((12, 128), jnp.int32),
+            pltpu.VMEM((1, 8 * UNIT), jnp.int32),
+            pltpu.VMEM((2, 128, 128), BF16),
             pltpu.VMEM((count, width), BF16),
             pltpu.VMEM((8 * UNIT, width), BF16),
             pltpu.VMEM((8, PER, width), BF16),
@@ -268,19 +336,17 @@
             pltpu.VMEM((512, 512), F32),
             pltpu.VMEM((512, 512), F32),
             pltpu.VMEM((8, *tile), F32),
-            pltpu.VMEM((4, *tile), F32),
-            pltpu.VMEM((4, *tile), F32),
-            pltpu.VMEM((4, *tile), F32),
+            pltpu.VMEM((8, *tile), F32),
             pltpu.VMEM(tile, F32),
             pltpu.VMEM((4, *tile), F32),
             pltpu.VMEM(tile, F32),
             pltpu.VMEM((8, *tile), F32),
-            pltpu.VMEM(tile, F32),
+            pltpu.VMEM((8, 16, 128), F32),
         ]
-        + [dma((4,)), dma((8,)), dma((8,)), dma((4,)), dma((4,)), dma((4, 4)), dma((4, 4)), dma((4, 4)), dma((4, 4))]
-        + [dma((21,)), dma((21,))],
+        + [dma((2,)), dma((4,)), dma((8,)), dma((8,)), dma((4,)), dma((4,)), dma((4, 4)), dma((4, 4)), dma((4, 4)), dma((4, 4))]
+        + [dma((28,)), dma((28,))],
         compiler_params=pltpu.CompilerParams(
-            collective_id=1, has_side_effects=True, vmem_limit_bytes=50 << 20
+            collective_id=1, has_side_effects=True, vmem_limit_bytes=67_043_328
         ),
         name="ranking_losses",
     )(queries, candidates, targets)
@@ -294,31 +360,9 @@
     return jnp.concatenate([top, total, picked, jnp.zeros((2, 128), F32)], axis=0)
 
 
-def in_place_order(targets):
-    t = targets.reshape(8, 4, 4, 2, PER)
-    low = t[:, :, :, 0].transpose(2, 1, 0, 3).reshape(4, UNIT)
-    high = t[:, :, :, 1].transpose(1, 2, 0, 3).reshape(4, UNIT)
-    return jnp.stack([low, high])
-
-
-def in_query_order(units):
-    low = units[:4].reshape(4, 4, 8, PER).transpose(2, 1, 0, 3)
-    high = units[4:].reshape(4, 4, 8, PER).transpose(2, 0, 1, 3)
-    return jnp.stack([low, high], axis=3).reshape(-1)
-
-
 def on_device(queries, candidates, targets):
-    z, u, v, c = place()
-    owner = z * 32 + lax.axis_index("shard")
-    t = in_place_order(targets - owner * candidates.shape[0])
-    slots = [None] * 8
-    for far in range(4):
-        slots[OWN[far]] = t[c, (u + far) % 4]
-        slots[OTHER[far]] = t[1 - c, (v + far) % 4]
-    out = all_losses(queries, candidates, jnp.concatenate(slots)[None])
-    units = jnp.concatenate([out[:, 0], out[:, 1, 64:]], axis=1)
-    losses = in_query_order(units)
-    return losses, jnp.mean(losses)
+    losses, mean = all_losses(queries, candidates, targets.reshape(12, 128))
+    return losses.reshape(-1), mean[0, 0]
 
 
 def solution(mesh):

time: 69 us -> 63.6 us (0.922)
  Pallas kernels: 61.2 us -> 59.7 us
  other arithmetic: 1.41 us -> 0 us
  local copies, waits for them, and re-layouts: 2.62 us -> 1.3 us
  between operations: 3.43 us -> 2.4 us
    pallas_call x1, Pallas kernels: 61.2 us -> 59.7 us  [all_losses(): pl.pallas_call(loss_kernel, out_shape=(jax.ShapeDtypeStruct((12, 128), F3...]
    reshape x5 -> x0, local copies, waits for them, and re-layouts: 1.23 us -> none  [the longest x1 0.8 us: in_query_order(): return jnp.stack([low, high], axis=3).reshape(-1)]
    sub x1 -> x0, other arithmetic: 0.7 us -> none  [on_device(): t = in_place_order(targets - owner * candidates.shape[0])]
    reduce_sum x1 -> x0, other arithmetic: 0.69 us -> none  [on_device(): return (losses, jnp.mean(losses))]
where the time goes in v3:
time: 63.6 us; the launch traced here: 63.4 us
  Pallas kernels  59.7 us (94%)
  between operations  2.4 us (4%)
  local copies, waits for them, and re-layouts  1.3 us (2%)
    pallas_call x1, Pallas kernels, all_losses(): pl.pallas_call(loss_kernel, out_shape=(jax.ShapeDtypeStruct((12, 128), F3...  59.7 us
    unnamed x1, local copies, waits for them, and re-layouts  1.3 us

profile of v3, /device:TPU:1, one launch (start us, length us, event | category | flops | bytes accessed | tf_op | source)
XLA Modules:
  0.0 63.4 jit_solution(634458224131154310)
XLA Ops:
  0.6 59.7 %ranking_losses.1 = (f32[12,128]{1,0:T(8,128)}, f32[1,1]{1,0:T(1,128)}) custom-call(bf16[6,1024]{1,0:T(8,128)(2,1)} %q_hbm.1, bf16[4096,1024]{1,0:T(8,128)(2,1)} %c_hbm.1, s32[12,128]{1,0:T(8,128)} %bitcast.3), custom_call_target="tpu_custom_call" | custom-call | tf_op jit(solution)/shard_map/ranking_losses/pallas_call | solution.py:318
  60.4 1.3 %copy.7 = f32[1536]{0:T(1024)} copy(f32[1536]{0:T(1024)} %bitcast.4) | data formatting | bytes 12288

commit v4 on v3

--- a/solution.py
+++ b/solution.py
@@ -14,10 +14,8 @@
 PER = 6
 BLOCK = 48
 UNIT = 192
-OWN = {0: 0, 1: 2, 3: 3, 2: 6}
-OTHER = {0: 1, 1: 4, 3: 5, 2: 7}
 NEAR_FIRST = (1, 3, 2)
-RELAYED_BY = (1, 3, 1, 3)
+RELAYED_BY = (1, 3, None, 1)
 BATCHES = ((0, 256), (256, 512), (768, 512), (1280, 256))
 
 
@@ -34,6 +32,14 @@
     x = v * (1 - c) + u * c
     y = u * (1 - c) + v * c
     return (z, (x * 4 + y) * 2 + c)
+
+
+def own_slot(far, c):
+    return {0: 0, 1: 4 - 2 * c, 3: 5 - 2 * c, 2: 6}[far]
+
+
+def other_slot(far, c):
+    return {0: 1, 1: 2 + 2 * c, 3: 3 + 2 * c, 2: 7}[far]
 
 
 def rows_of(slot, v):
@@ -97,7 +103,7 @@
     return (total[0:16] + total[16:32]) + total[32:48]
 
 
-def scored_batch(c_buf, q_ref, t_ref, first, cols, s0, s1):
+def scored_batch(c_buf, q_ref, t_ref, first, cols, s0, s1, between):
     rows = s0.shape[0]
     blocks = c_buf.shape[0] // rows
     groups = rows // 8
@@ -133,7 +139,14 @@
     old = jnp.full((8, cols), LOW, F32)
     zero = jnp.zeros((8, cols), F32)
     carry = (old, peak(scored(0, s0), old), zero, zero)
-    old, new, total, picked = lax.fori_loop(0, blocks // 2 - 1, step, carry)
+    pairs = blocks // 2 - 1
+    for k, handle in enumerate(between):
+        if handle is not None:
+            handle()
+        if k < pairs:
+            carry = lax.fori_loop(k, k + 1, step, carry)
+    carry = lax.fori_loop(min(len(between), pairs), pairs, step, carry)
+    old, new, total, picked = carry
     newer = peak(scored(blocks - 1, s1), new)
     total, picked = take(s0, blocks - 2, old, new, total, picked)
     total, picked = take(s1, blocks - 1, new, newer, total, picked)
@@ -175,7 +188,6 @@
     for load in loads:
         load.start()
     ask.wait()
-    sent = []
 
     def copy(src, dst, send, recv, to):
         return pltpu.make_async_remote_copy(
@@ -183,16 +195,12 @@
         )
 
     def start(*args):
-        one = copy(*args)
-        one.start()
-        sent.append(one)
+        copy(*args).start()
 
     for d in (4, 3, 5, 2, 6, 1, 7):
         start(first.at[z], first.at[z], send1.at[d], recv1.at[d], column[d - 1])
-    slots = [None] * 8
-    for far in range(4):
-        slots[OWN[far]] = c, (u + far) % 4
-        slots[OTHER[far]] = 1 - c, (v + far) % 4
+    slots = [(c, u), (1 - c, v), (1, (x + 1) % 4), (1, (x + 3) % 4)]
+    slots += [(0, (y + 1) % 4), (0, (y + 3) % 4), (c, (u + 2) % 4), (1 - c, (v + 2) % 4)]
     ask_t.wait()
     owner = z * 32 + lax.axis_index("shard")
     t_ref[...] = own_targets(t_nat[...], owner, c_buf.shape[0], slots)
@@ -205,22 +213,22 @@
     all_ref[rows_of(0, v), :] = block.astype(BF16)
 
     def to_partner(far, d):
-        held = all_ref.at[rows_of(OWN[far], (v + 4 - d) % 4)]
-        there = all_ref.at[rows_of(OTHER[far], (v + 4 - d) % 4)]
+        held = all_ref.at[rows_of(own_slot(far, c), (v + 4 - d) % 4)]
+        there = all_ref.at[rows_of(other_slot(far, 1 - c), (v + 4 - d) % 4)]
         start(held, there, sendp.at[far, d], recvp.at[far, d], partner)
 
     def along(e, d):
         held = all_ref.at[rows_of(0, (v + 4 - d) % 4)]
-        there = all_ref.at[rows_of(OWN[(4 - e) % 4], (v + 4 - d) % 4)]
+        there = all_ref.at[rows_of(own_slot((4 - e) % 4, c), (v + 4 - d) % 4)]
         start(held, there, send3.at[e, d], recv3.at[e, d], along_u[e])
 
     def arrived_along(e, d):
-        here = all_ref.at[rows_of(OWN[(4 - e) % 4], (v + 4 - d) % 4)]
+        here = all_ref.at[rows_of(own_slot((4 - e) % 4, c), (v + 4 - d) % 4)]
         copy(here, here, send3.at[e, d], recv3.at[e, d], along_u[e]).wait_recv()
 
     def from_partner(far):
         for d in range(4):
-            here = all_ref.at[rows_of(OTHER[far], (u + 4 - d) % 4)]
+            here = all_ref.at[rows_of(other_slot(far, c), (u + 4 - d) % 4)]
             copy(here, here, sendp.at[far, d], recvp.at[far, d], partner).wait_recv()
 
     own = all_ref.at[rows_of(0, v)]
@@ -235,33 +243,47 @@
         to_partner(0, d)
         along(1, d)
         along(3, d)
+    along(2, 2)
+
+    def near_blocks(*ds):
+        for d in ds:
+            for e in (1, 3):
+                arrived_along(e, d)
+                if e == RELAYED_BY[d]:
+                    held = all_ref.at[rows_of(own_slot((4 - e) % 4, c), (v + 4 - d) % 4)]
+                    there = all_ref.at[rows_of(own_slot(2, c), (v + 4 - d) % 4)]
+                    start(held, there, send3.at[2, d], recv3.at[2, d], along_u[e])
+                to_partner((4 - e) % 4, d)
+
+    def on_core(core, handle, *ds):
+        pl.when(c == core)(lambda: handle(*ds))
+
+    def near_from_partner():
+        from_partner(1)
+        from_partner(3)
+
+    on_core(1, near_blocks, 0, 1, 3, 2)
+    on_core(0, near_blocks, 0)
     for load in loads:
         load.wait()
     from_partner(0)
 
     results = []
 
-    def run(k):
+    def run(k, between=()):
         begin, cols = BATCHES[k]
         held = (narrow0, narrow1) if cols == narrow0.shape[1] else (wide0, wide1)
-        results.append(scored_batch(c_buf, all_ref, t_ref, begin, cols, *held))
+        results.append(scored_batch(c_buf, all_ref, t_ref, begin, cols, *held, between))
 
     run(0)
-    for d in (0, 1, 3, 2):
-        for e in (1, 3):
-            arrived_along(e, d)
-            if e == RELAYED_BY[d]:
-                held = all_ref.at[rows_of(OWN[(4 - e) % 4], (v + 4 - d) % 4)]
-                there = all_ref.at[rows_of(OWN[2], (v + 4 - d) % 4)]
-                start(held, there, send3.at[2, d], recv3.at[2, d], along_u[e])
-            to_partner((4 - e) % 4, d)
-    run(1)
+    on_core(0, near_blocks, 1)
+    on_core(0, near_from_partner)
+    run(1, (None, lambda: on_core(0, near_blocks, 3), lambda: on_core(0, near_blocks, 2)))
     for d in (0, 1, 3, 2):
         arrived_along(2, d)
         to_partner(2, d)
-    from_partner(1)
-    from_partner(3)
-    run(2)
+    on_core(1, near_from_partner)
+    run(2, (None, None, None))
     from_partner(2)
     run(3)
 
@@ -307,8 +329,21 @@
     every = ((shared[0] + shared[1]) + (shared[2] + shared[3])) + ((shared[4] + shared[5]) + (shared[6] + shared[7]))
     o_ref[...] = every[0:12]
     mean_ref[...] = jnp.sum(every, keepdims=True) * (1.0 / (8 * UNIT))
-    for one in sent:
-        one.wait_send()
+    for d in range(1, 8):
+        copy(first.at[z], first.at[z], send1.at[d], recv1.at[d], partner).wait_send()
+    for d in range(4):
+        if d:
+            copy(own, own, send2.at[d], recv2.at[d], partner).wait_send()
+        for e in range(4):
+            copy(own, own, sendp.at[e, d], recvp.at[e, d], partner).wait_send()
+            if e:
+                copy(own, own, send3.at[e, d], recv3.at[e, d], partner).wait_send()
+    for k in range(1, 8):
+        if k < 4:
+            copy(at_y, at_y, sends.at[3 + k], recvs.at[3 + k], partner).wait_send()
+        copy(at_z, at_z, sends.at[6 + k], recvs.at[6 + k], partner).wait_send()
+        copy(at_z, at_z, sends.at[13 + k], recvs.at[13 + k], partner).wait_send()
+        copy(shared.at[0], shared.at[0], sends.at[20 + k], recvs.at[20 + k], partner).wait_send()
 
 
 def all_losses(queries, candidates, targets):
@@ -346,7 +381,7 @@
         + [dma((2,)), dma((4,)), dma((8,)), dma((8,)), dma((4,)), dma((4,)), dma((4, 4)), dma((4, 4)), dma((4, 4)), dma((4, 4))]
         + [dma((28,)), dma((28,))],
         compiler_params=pltpu.CompilerParams(
-            collective_id=1, has_side_effects=True, vmem_limit_bytes=67_043_328
+            collective_id=1, has_side_effects=True, vmem_limit_bytes=50 << 20
         ),
         name="ranking_losses",
     )(queries, candidates, targets)
@@ -361,7 +396,8 @@
 
 
 def on_device(queries, candidates, targets):
-    losses, mean = all_losses(queries, candidates, targets.reshape(12, 128))
+    held = (queries, candidates, targets.reshape(12, 128))
+    losses, mean = all_losses(*(pltpu.with_memory_space_constraint(a, pltpu.HBM) for a in held))
     return losses.reshape(-1), mean[0, 0]
 
 

time: 63.6 us -> 60.3 us (0.948)
  Pallas kernels: 59.7 us -> 57.3 us
  local copies, waits for them, and re-layouts: 1.3 us -> 0.6 us
    pallas_call x1, Pallas kernels: 59.7 us -> 57.3 us  [all_losses(): pl.pallas_call(loss_kernel, out_shape=(jax.ShapeDtypeStruct((12, 128), F3...]
    unnamed x1, local copies, waits for them, and re-layouts: 1.3 us -> 0.6 us
where the time goes in v4:
time: 60.3 us; the launch traced here: 60.2 us
  Pallas kernels  57.3 us (95%)
  between operations  2.33 us (4%)
    pallas_call x1, Pallas kernels, all_losses(): pl.pallas_call(loss_kernel, out_shape=(jax.ShapeDtypeStruct((12, 128), F3...  57.3 us

profile of v4, /device:TPU:1, one launch (start us, length us, event | category | flops | bytes accessed | tf_op | source)
XLA Modules:
  0.0 60.2 jit_solution(4189982273347825096)
XLA Ops:
  0.6 57.3 %ranking_losses.1 = (f32[12,128]{1,0:T(8,128)S(1)}, f32[1,1]{1,0:T(1,128)}) custom-call(bf16[6,1024]{1,0:T(8,128)(2,1)} %q_hbm.1, bf16[4096,1024]{1,0:T(8,128)(2,1)} %c_hbm.1, s32[12,128]{1,0:T(8,128)} %bitcast.4), custom_call_target="tpu_custom_call" | custom-call | tf_op jit(solution)/shard_map/ranking_losses/pallas_call | solution.py:353
  57.9 0.6 copy.7

commit v5 on v4

--- a/solution.py
+++ b/solution.py
@@ -103,7 +103,7 @@
     return (total[0:16] + total[16:32]) + total[32:48]
 
 
-def scored_batch(c_buf, q_ref, t_ref, first, cols, s0, s1, between):
+def scored_batch(c_buf, q_ref, t_ref, first, cols, s0, s1, between, before):
     rows = s0.shape[0]
     blocks = c_buf.shape[0] // rows
     groups = rows // 8
@@ -139,6 +139,7 @@
     old = jnp.full((8, cols), LOW, F32)
     zero = jnp.zeros((8, cols), F32)
     carry = (old, peak(scored(0, s0), old), zero, zero)
+    before()
     pairs = blocks // 2 - 1
     for k, handle in enumerate(between):
         if handle is not None:
@@ -149,10 +150,14 @@
     old, new, total, picked = carry
     newer = peak(scored(blocks - 1, s1), new)
     total, picked = take(s0, blocks - 2, old, new, total, picked)
-    total, picked = take(s1, blocks - 1, new, newer, total, picked)
-    top = jnp.max(newer, axis=0, keepdims=True)
-    total = jnp.sum(total * jnp.exp(newer - top), axis=0, keepdims=True)
-    return top, total, jnp.sum(picked, axis=0, keepdims=True)
+
+    def finish():
+        last, found = take(s1, blocks - 1, new, newer, total, picked)
+        top = jnp.max(newer, axis=0, keepdims=True)
+        last = jnp.sum(last * jnp.exp(newer - top), axis=0, keepdims=True)
+        return top, last, jnp.sum(found, axis=0, keepdims=True)
+
+    return finish
 
 
 def loss_kernel(
@@ -269,11 +274,16 @@
     from_partner(0)
 
     results = []
+    ends = []
+
+    def end():
+        if ends:
+            results.append(ends.pop()())
 
     def run(k, between=()):
         begin, cols = BATCHES[k]
         held = (narrow0, narrow1) if cols == narrow0.shape[1] else (wide0, wide1)
-        results.append(scored_batch(c_buf, all_ref, t_ref, begin, cols, *held, between))
+        ends.append(scored_batch(c_buf, all_ref, t_ref, begin, cols, *held, between, end))
 
     run(0)
     on_core(0, near_blocks, 1)
@@ -286,6 +296,7 @@
     run(2, (None, None, None))
     from_partner(2)
     run(3)
+    end()
 
     lines = [jnp.concatenate(parts, axis=1) for parts in zip(*results)]
     for slot, (colour, there) in enumerate(slots):

time: 60.3 us -> 60 us (level)
  no operation moved by 1% of the time
where the time goes in v5:
time: 60 us; the launch traced here: 59.9 us
  Pallas kernels  57 us (95%)
  between operations  2.33 us (4%)
  local copies, waits for them, and re-layouts  0.6 us (1%)
    pallas_call x1, Pallas kernels, all_losses(): pl.pallas_call(loss_kernel, out_shape=(jax.ShapeDtypeStruct((12, 128), F3...  57 us

profile of v5, /device:TPU:1, one launch (start us, length us, event | category | flops | bytes accessed | tf_op | source)
XLA Modules:
  0.0 59.9 jit_solution(5710845123883716250)
XLA Ops:
  0.6 57.0 %ranking_losses.1 = (f32[12,128]{1,0:T(8,128)S(1)}, f32[1,1]{1,0:T(1,128)}) custom-call(bf16[6,1024]{1,0:T(8,128)(2,1)} %q_hbm.1, bf16[4096,1024]{1,0:T(8,128)(2,1)} %c_hbm.1, s32[12,128]{1,0:T(8,128)} %bitcast.4), custom_call_target="tpu_custom_call" | custom-call | tf_op jit(solution)/shard_map/ranking_losses/pallas_call | solution.py:364
  57.7 0.6 %copy.7 = f32[1536]{0:T(1024)} copy(f32[1536]{0:T(1024)S(1)} %bitcast.3) | data formatting | bytes 12288

commit v6 on v5

--- a/solution.py
+++ b/solution.py
@@ -15,7 +15,7 @@
 BLOCK = 48
 UNIT = 192
 NEAR_FIRST = (1, 3, 2)
-RELAYED_BY = (1, 3, None, 1)
+RELAYED_BY = ((1, 3, None, 1), (1, 3, 3, 1))
 BATCHES = ((0, 256), (256, 512), (768, 512), (1280, 256))
 
 
@@ -248,22 +248,22 @@
         to_partner(0, d)
         along(1, d)
         along(3, d)
-    along(2, 2)
-
-    def near_blocks(*ds):
+    pl.when(c == 0)(lambda: along(2, 2))
+
+    def near_blocks(core, *ds):
         for d in ds:
             for e in (1, 3):
                 arrived_along(e, d)
-                if e == RELAYED_BY[d]:
+                if e == RELAYED_BY[core][d]:
                     held = all_ref.at[rows_of(own_slot((4 - e) % 4, c), (v + 4 - d) % 4)]
                     there = all_ref.at[rows_of(own_slot(2, c), (v + 4 - d) % 4)]
                     start(held, there, send3.at[2, d], recv3.at[2, d], along_u[e])
                 to_partner((4 - e) % 4, d)
 
     def on_core(core, handle, *ds):
-        pl.when(c == core)(lambda: handle(*ds))
-
-    def near_from_partner():
+        pl.when(c == core)(lambda: handle(core, *ds))
+
+    def near_from_partner(core):
         from_partner(1)
         from_partner(3)
 

time: 60 us -> 60 us (level)
  no operation moved by 1% of the time
where the time goes in v6:
time: 60 us; the launch traced here: 59.9 us
  Pallas kernels  57 us (95%)
  between operations  2.33 us (4%)
  local copies, waits for them, and re-layouts  0.6 us (1%)
    pallas_call x1, Pallas kernels, all_losses(): pl.pallas_call(loss_kernel, out_shape=(jax.ShapeDtypeStruct((12, 128), F3...  57 us

profile of v6, /device:TPU:1, one launch (start us, length us, event | category | flops | bytes accessed | tf_op | source)
XLA Modules:
  0.0 59.9 jit_solution(15595440740460625486)
XLA Ops:
  0.6 57.0 %ranking_losses.1 = (f32[12,128]{1,0:T(8,128)S(1)}, f32[1,1]{1,0:T(1,128)}) custom-call(bf16[6,1024]{1,0:T(8,128)(2,1)} %q_hbm.1, bf16[4096,1024]{1,0:T(8,128)(2,1)} %c_hbm.1, s32[12,128]{1,0:T(8,128)} %bitcast.4), custom_call_target="tpu_custom_call" | custom-call | tf_op jit(solution)/shard_map/ranking_losses/pallas_call | solution.py:364
  57.6 0.6 %copy.7 = f32[1536]{0:T(1024)} copy(f32[1536]{0:T(1024)S(1)} %bitcast.3) | data formatting | bytes 12288
